TPU v7x, 32 devices: a whole 2x2x4 slice. The times are simulated.
32 devices in a mesh: bank: 4 (over y, x), zero: 8 (over z, core).
Axes of the slice: x: 2, y: 2, z: 4, core: 2. Of those that a mesh axis runs over, the one named last changes fastest.
Arguments:
- w_down: float32 [64, 1024, 2048], P('bank', None, 'zero'), may hold values from -0.25 to 0.25
- avg_down: bfloat16 [64, 1024, 2048], P('bank', None, 'zero'), may hold values from -0.09375 to 0.09375
- router_weight: float32 [2048, 64], P('zero', 'bank'), may hold values from -0.125 to 0.125
- router_gain: float32 [2048], P('zero'), may hold values from 0.25 to 1.75
Outputs:
- serve_down: bfloat16 [64, 1024, 2048], P('bank')
- scale_down: float32 [64, 1024], P('bank')
- serve_router: bfloat16 [2048, 64], replicated
All inputs are finite; a program needn't handle non-finite values.
Results may differ from a plain program's by a relative error of at most 0.001.
Values may be sent and summed in bfloat16 or wider, within the bound.
A program may use at most 256 MiB of HBM per device.

v0:
```python
import jax
import jax.numpy as jnp
from jax import lax
from jax.sharding import PartitionSpec as P


def shards(w_down, avg_down, router_weight, router_gain):
    fresh_down = w_down + avg_down.astype(jnp.float32)
    total_down = lax.psum(jnp.sum(fresh_down * fresh_down, axis=2), "zero")
    scale_down = jnp.sqrt(total_down)
    narrow_down = (fresh_down / jnp.expand_dims(scale_down, 2)).astype(jnp.bfloat16)
    serve_down = lax.all_gather(narrow_down, "zero", axis=2, tiled=True)
    part_router = (router_weight * router_gain[:, None]).astype(jnp.bfloat16)
    row_router = lax.all_gather(part_router, "zero", axis=0, tiled=True)
    serve_router = lax.all_gather(row_router, "bank", axis=1, tiled=True)
    return (serve_down, scale_down, serve_router)


def solution(mesh):
    return jax.shard_map(
        shards,
        mesh=mesh,
        in_specs=(P("bank", None, "zero"), P("bank", None, "zero"), P("zero", "bank"), P("zero")),
        out_specs=(P("bank", None, None), P("bank", None), P()),
        check_vma=False,
    )
```

profile of v0, /device:TPU:25, one launch (start us, length us, event | category | flops | bytes accessed | tf_op | source)
XLA Modules:
  0.0 708.1 jit_solution(10193368544461576350)
XLA Ops:
  7.2 0.0 all-reduce.2.cloned.1.call-start
  7.2 9.7 %multiply_reduce_fusion = f32[16,1024]{1,0:T(8,128)} fusion(f32[16,1024,256]{2,1,0:T(8,128)} %param.4, bf16[16,1024,256]{2,1,0:T(8,128)(2,1)} %param.5), kind=kLoop, calls=%fused_computation.1 | loop fusion | flops 16760832 | bytes 25231360 | tf_op jit(solution)/shard_map/reduce_sum | solution.py:9
  17.0 0.0 all-reduce.2.cloned.1.call-update
  17.0 0.0 all-gather.2.cloned.1.call-start
  17.0 53.1 %all-reduce.2.cloned.1.call-done = f32[16,1024]{1,0:T(8,128)} async-done(((f32[16,1024]{1,0:T(8,128)}), f32[16,1024]{1,0:T(8,128)}) %all-reduce.2.cloned.1.call-update) | async-done | bytes 65552 | tf_op jit(solution)/shard_map/psum | solution.py:9
  70.2 0.9 sqrt.3
  71.0 0.0 copy-start
  71.0 0.0 copy-start.1
  71.0 0.0 copy-start.2
  71.1 12.0 %divide_convert_fusion = bf16[16,1024,256]{2,1,0:T(8,128)(2,1)} fusion(f32[16,1024,256]{2,1,0:T(8,128)} %param.4, bf16[16,1024,256]{2,1,0:T(8,128)(2,1)} %param.5, f32[16,1024]{1,0:T(8,128)S(1)} %sqrt.3), kind=kLoop, calls=%fused_computation | loop fusion | flops 16777216 | bytes 33619968 | tf_op jit(solution)/shard_map/convert_element_type | solution.py:11
  83.1 0.0 copy-done
  83.1 0.0 all-gather.2.cloned.1.call-update
  83.1 0.0 copy-done.1
  83.1 0.0 copy-done.2
  83.1 15.2 %all_gather.10 = bf16[2048,16]{0,1:T(8,128)(2,1)S(1)} all-gather(bf16[256,16]{0,1:T(8,128)(2,1)S(1)} %multiply_convert_fusion), channel_id=1, replica_groups=mesh['bank'=4,'zero'=8] {'zero'}, dimensions={0}, use_global_device_ids=true | all-gather | bytes 73728 | tf_op jit(solution)/shard_map/all_gather | solution.py:14
  98.3 7.3 %all_gather.11 = bf16[2048,64]{0,1:T(8,128)(2,1)S(1)} all-gather(bf16[2048,16]{0,1:T(8,128)(2,1)S(1)} %all_gather.10), channel_id=1, replica_groups=mesh['bank'=4,'zero'=8] {'bank'}, dimensions={1}, use_global_device_ids=true | all-gather | bytes 327680 | tf_op jit(solution)/shard_map/all_gather | solution.py:15
  105.7 550.9 %all-gather.2.cloned.1.call-done = bf16[16,1024,2048]{2,1,0:T(8,128)(2,1)} async-done(((bf16[16,1024,256]{2,1,0:T(8,128)(2,1)}), bf16[16,1024,2048]{2,1,0:T(8,128)(2,1)}) %all-gather.2.cloned.1.call-update) | async-done | bytes 67108880 | tf_op jit(solution)/shard_map/all_gather | solution.py:12
  656.6 44.0 %copy.10 = bf16[16,1024,2048]{2,1,0:T(8,128)(2,1)} copy(bf16[16,1024,2048]{2,1,0:T(8,128)(2,1)} %all-gather.2.cloned.1.call-done) | data formatting | bytes 134217728
  700.6 0.7 copy.11
  (1 shorter events, 0.0 us)
Async XLA Ops:
  7.2 63.0 %all-reduce.2.cloned.1.call-start = ((), (), s32[]{:S(2)}) async-start(), calls=%async_computation | async-start | bytes 131072 | tf_op jit(solution)/shard_map/psum | solution.py:9
  17.0 639.6 %all-gather.2.cloned.1.call-start = ((), (), s32[]{:S(2)}) async-start(), calls=%async_computation.1 | async-start | bytes 75497472 | tf_op jit(solution)/shard_map/all_gather | solution.py:12
  71.0 12.1 %copy-start = (f32[16,1024]{1,0:T(8,128)}, f32[16,1024]{1,0:T(8,128)S(1)}, u32[]{:S(2)}) copy-start(f32[16,1024]{1,0:T(8,128)S(1)} %sqrt.3) | copy-start | bytes 196612
  71.0 12.1 %copy-start.1 = (f32[256,16]{0,1:T(8,128)S(1)}, f32[256,16]{0,1:T(8,128)}, u32[]{:S(2)}) copy-start(f32[256,16]{0,1:T(8,128)} %param.6) | copy-start | bytes 49156
  71.0 12.1 %copy-start.2 = (f32[256]{0:T(256)S(1)}, f32[256]{0:T(256)}, u32[]{:S(2)}) copy-start(f32[256]{0:T(256)} %param.7) | copy-start | bytes 3076
Sparse Core Ops, SparseCore 0:
  17.1 53.0 all-reduce.1
  83.2 573.2 all-gather.1
where the time goes:
time: 708 us
  waiting for transfers between devices  604 us (85%)
  local copies, waits for them, and re-layouts  45.6 us (6%)
  blocking collectives  22.5 us (3%)
  other arithmetic  21.8 us (3%)
  between operations  14.1 us (2%)
    all_gather x1, waiting for transfers between devices, shards(): serve_down = lax.all_gather(narrow_down, 'zero', axis=2, tiled=True)  551 us
    psum x1, waiting for transfers between devices, shards(): total_down = lax.psum(jnp.sum(fresh_down * fresh_down, axis=2), 'zero')  53.1 us
    unnamed x8, local copies, waits for them, and re-layouts  44.8 us
    all_gather x1, blocking collectives, shards(): row_router = lax.all_gather(part_router, 'zero', axis=0, tiled=True)  15.2 us
  transfers between devices with their start and end apart: 2, of which 2 were waited for; matrix products, arithmetic and copies ran while one was open for 0% of the time, Pallas kernels for 0%

commit v1 on v0

--- a/solution.py
+++ b/solution.py
@@ -9,7 +9,8 @@
     total_down = lax.psum(jnp.sum(fresh_down * fresh_down, axis=2), "zero")
     scale_down = jnp.sqrt(total_down)
     narrow_down = (fresh_down / jnp.expand_dims(scale_down, 2)).astype(jnp.bfloat16)
-    serve_down = lax.all_gather(narrow_down, "zero", axis=2, tiled=True)
+    blocks = lax.all_gather(narrow_down, "zero")
+    serve_down = jnp.concatenate(blocks, axis=2)
     part_router = (router_weight * router_gain[:, None]).astype(jnp.bfloat16)
     row_router = lax.all_gather(part_router, "zero", axis=0, tiled=True)
     serve_router = lax.all_gather(row_router, "bank", axis=1, tiled=True)

time: 708 us -> 703 us (level)
  waiting for transfers between devices: 604 us -> 594 us
    reshape x0 -> x1, local copies, waits for them, and re-layouts: none -> 44.3 us  [shards(): serve_down = jnp.concatenate(blocks, axis=2)]
    unnamed x8 -> x7, local copies, waits for them, and re-layouts: 44.8 us -> 0.72 us
    all_gather x1, waiting for transfers between devices: 551 us -> 541 us  [shards(): blocks = lax.all_gather(narrow_down, 'zero')]
where the time goes in v1:
time: 703 us; the launch traced here: 698 us
  waiting for transfers between devices  594 us (84%)
  local copies, waits for them, and re-layouts  45.9 us (7%)
  blocking collectives  22.5 us (3%)
  other arithmetic  21.8 us (3%)
  between operations  14.1 us (2%)
    all_gather x1, waiting for transfers between devices, shards(): blocks = lax.all_gather(narrow_down, 'zero')  541 us
    psum x1, waiting for transfers between devices, shards(): total_down = lax.psum(jnp.sum(fresh_down * fresh_down, axis=2), 'zero')  53.1 us
    reshape x1, local copies, waits for them, and re-layouts, shards(): serve_down = jnp.concatenate(blocks, axis=2)  44.3 us
    all_gather x1, blocking collectives, shards(): row_router = lax.all_gather(part_router, 'zero', axis=0, tiled=True)  15.2 us
  transfers between devices with their start and end apart: 2, of which 2 were waited for; matrix products, arithmetic and copies ran while one was open for 0% of the time, Pallas kernels for 0%

profile of v1, /device:TPU:25, one launch (start us, length us, event | category | flops | bytes accessed | tf_op | source)
XLA Modules:
  0.0 698.2 jit_solution(3893677561080732542)
XLA Ops:
  7.2 0.0 all-reduce.2.cloned.1.call-start
  7.2 9.7 %multiply_reduce_fusion = f32[16,1024]{1,0:T(8,128)} fusion(f32[16,1024,256]{2,1,0:T(8,128)} %param.4, bf16[16,1024,256]{2,1,0:T(8,128)(2,1)} %param.5), kind=kLoop, calls=%fused_computation.1 | loop fusion | flops 16760832 | bytes 25231360 | tf_op jit(solution)/shard_map/reduce_sum | solution.py:9
  17.0 0.0 all-reduce.2.cloned.1.call-update
  17.0 0.0 all-gather.3.cloned.1.call-start
  17.0 53.1 %all-reduce.2.cloned.1.call-done = f32[16,1024]{1,0:T(8,128)} async-done(((f32[16,1024]{1,0:T(8,128)}), f32[16,1024]{1,0:T(8,128)}) %all-reduce.2.cloned.1.call-update) | async-done | bytes 65552 | tf_op jit(solution)/shard_map/psum | solution.py:9
  70.2 0.9 sqrt.3
  71.0 0.0 copy-start
  71.0 0.0 copy-start.1
  71.0 0.0 copy-start.2
  71.1 12.0 %divide_convert_fusion = bf16[16,1024,256]{2,1,0:T(8,128)(2,1)} fusion(f32[16,1024,256]{2,1,0:T(8,128)} %param.4, bf16[16,1024,256]{2,1,0:T(8,128)(2,1)} %param.5, f32[16,1024]{1,0:T(8,128)S(1)} %sqrt.3), kind=kLoop, calls=%fused_computation | loop fusion | flops 16777216 | bytes 33619968 | tf_op jit(solution)/shard_map/convert_element_type | solution.py:11
  83.1 0.0 copy-done
  83.1 0.0 all-gather.3.cloned.1.call-update
  83.1 0.0 copy-done.1
  83.1 0.0 copy-done.2
  83.1 15.2 %all_gather.14 = bf16[2048,16]{0,1:T(8,128)(2,1)S(1)} all-gather(bf16[256,16]{0,1:T(8,128)(2,1)S(1)} %multiply_convert_fusion), channel_id=1, replica_groups=mesh['bank'=4,'zero'=8] {'zero'}, dimensions={0}, use_global_device_ids=true | all-gather | bytes 73728 | tf_op jit(solution)/shard_map/all_gather | solution.py:15
  98.3 7.3 %all_gather.15 = bf16[2048,64]{0,1:T(8,128)(2,1)S(1)} all-gather(bf16[2048,16]{0,1:T(8,128)(2,1)S(1)} %all_gather.14), channel_id=1, replica_groups=mesh['bank'=4,'zero'=8] {'bank'}, dimensions={1}, use_global_device_ids=true | all-gather | bytes 327680 | tf_op jit(solution)/shard_map/all_gather | solution.py:16
  105.7 540.6 %all-gather.3.cloned.1.call-done = bf16[128,1024,256]{2,1,0:T(8,128)(2,1)} async-done(((bf16[16,1024,256]{2,1,0:T(8,128)(2,1)}), bf16[128,1024,256]{2,1,0:T(8,128)(2,1)}) %all-gather.3.cloned.1.call-update) | async-done | bytes 67108880 | tf_op jit(solution)/shard_map/all_gather | solution.py:12
  646.3 44.3 %copy.9 = bf16[8,16,128,8,256]{4,3,0,2,1:T(8,128)(2,1)} copy(bf16[8,16,128,8,256]{4,3,2,1,0:T(8,128)(2,1)} %bitcast.3) | data formatting | bytes 134217728 | tf_op jit(solution)/shard_map/reshape | solution.py:13
  690.6 0.7 copy.12
  (1 shorter events, 0.0 us)
Async XLA Ops:
  7.2 63.0 %all-reduce.2.cloned.1.call-start = ((), (), s32[]{:S(2)}) async-start(), calls=%async_computation | async-start | bytes 131072 | tf_op jit(solution)/shard_map/psum | solution.py:9
  17.0 629.3 %all-gather.3.cloned.1.call-start = ((), (), s32[]{:S(2)}) async-start(), calls=%async_computation.1 | async-start | bytes 75497472 | tf_op jit(solution)/shard_map/all_gather | solution.py:12
  71.0 12.1 %copy-start = (f32[16,1024]{1,0:T(8,128)}, f32[16,1024]{1,0:T(8,128)S(1)}, u32[]{:S(2)}) copy-start(f32[16,1024]{1,0:T(8,128)S(1)} %sqrt.3) | copy-start | bytes 196612
  71.0 12.1 %copy-start.1 = (f32[256,16]{0,1:T(8,128)S(1)}, f32[256,16]{0,1:T(8,128)}, u32[]{:S(2)}) copy-start(f32[256,16]{0,1:T(8,128)} %param.6) | copy-start | bytes 49156
  71.0 12.1 %copy-start.2 = (f32[256]{0:T(256)S(1)}, f32[256]{0:T(256)}, u32[]{:S(2)}) copy-start(f32[256]{0:T(256)} %param.7) | copy-start | bytes 3076
Sparse Core Ops, SparseCore 0:
  17.1 53.0 all-reduce.1
  83.2 563.0 all-gather.2
